TPU v7x, 32 devices: a whole 2x2x4 slice. The times are simulated.
32 devices in a mesh: row: 8 (over z, core), col: 4 (over y, x).
Axes of the slice: x: 2, y: 2, z: 4, core: 2. Of those that a mesh axis runs over, the one named last changes fastest.
Arguments:
- right_sides: float32 [4, 1024, 4096], P(None, 'row', 'col'), may hold values from -6 to 6
- low_left: bfloat16 [6, 4096, 128], P(None, 'col'), may hold values from -0.25 to 0.25
- low_right: bfloat16 [6, 4096, 128], P(None, 'col'), may hold values from -0.09375 to 0.09375
- up_left: bfloat16 [6, 4096, 128], P(None, 'col'), may hold values from -0.25 to 0.25
- up_right: bfloat16 [6, 4096, 128], P(None, 'col'), may hold values from -0.09375 to 0.09375
- low_ranks: int32 [6], replicated, may hold values from 1 to 4
- up_ranks: int32 [6], replicated, may hold values from 1 to 4
- inv_lower: bfloat16 [4, 4096, 4096], P(None, 'col', 'row'), may hold values from -0.09375 to 0.09375
- inv_upper: bfloat16 [4, 4096, 4096], P(None, 'col', 'row'), may hold values from -0.09375 to 0.09375
Outputs:
- solution: float32 [4, 1024, 4096], P(None, 'row', 'col')
Inputs may be any that keep to these rules, and one draw needn't show every extreme that they name: `low_ranks`: factor columns beyond 32 times this value are padding with arbitrary values and must be masked out. `up_ranks`: factor columns beyond 32 times this value are padding with arbitrary values and must be masked out.
All inputs are finite; a program needn't handle non-finite values.
Results may differ from a plain program's by a relative error of at most 0.03.
Values may be sent and summed in bfloat16 or wider, within the bound.
A program may use at most 64 MiB of HBM per device.

v0:
```python
import jax
import jax.numpy as jnp
import numpy as np
from jax import lax
from jax.sharding import PartitionSpec as P

RBLK = 32


def rank_mask(ranks, pair_index, rank_cols):
    columns = jnp.arange(rank_cols, dtype=jnp.int32)
    return (columns[None, :] < RBLK * ranks[pair_index][:, None]).astype(jnp.float32)


def times_inverse(block, inverse):
    return lax.dot_general(
        block, inverse, (((1,), (1,)), ((), ())), preferred_element_type=jnp.float32
    )


def sum_terms(moved, inverse):
    return times_inverse(moved, inverse)


def shards(
    right_sides, low_left, low_right, up_left, up_right, low_ranks, up_ranks, inv_lower, inv_upper
):
    tile_count = right_sides.shape[0]
    rank_cols = low_left.shape[2]
    residual = right_sides
    forward = []
    for section in range(tile_count):
        rounded = residual[section].astype(jnp.bfloat16)
        whole = lax.all_gather(rounded, "col", axis=1, tiled=True)
        moved = lax.all_to_all(whole, "row", split_axis=1, concat_axis=0, tiled=True)
        solved = lax.psum_scatter(
            sum_terms(moved, inv_lower[section]).astype(jnp.bfloat16),
            "row",
            scatter_dimension=0,
            tiled=True,
        ).astype(jnp.float32)
        forward.append(solved)
        if section + 1 < tile_count:
            pair_index = np.array(
                [tile * (tile - 1) // 2 + section for tile in range(section + 1, tile_count)],
                dtype=np.int32,
            )
            projections = jnp.einsum(
                "nw,mwr->mnr",
                solved.astype(jnp.bfloat16),
                low_right[pair_index],
                preferred_element_type=jnp.float32,
            )
            leading = lax.psum(projections[:1].astype(jnp.bfloat16), "col").astype(jnp.float32)
            if section + 2 < tile_count:
                remaining = lax.psum(projections[1:].astype(jnp.bfloat16), "col").astype(
                    jnp.float32
                )
                summed = jnp.concatenate([leading, remaining], axis=0)
            else:
                summed = leading
            masked = (summed * rank_mask(low_ranks, pair_index, rank_cols)[:, None, :]).astype(
                jnp.bfloat16
            )
            update = jnp.einsum(
                "mnr,mwr->mnw", masked, low_left[pair_index], preferred_element_type=jnp.float32
            )
            residual = residual.at[section + 1 :].add(-update)
    state = jnp.stack(forward)
    solutions = [None] * tile_count
    for section in range(tile_count - 1, -1, -1):
        rounded = state[section].astype(jnp.bfloat16)
        whole = lax.all_gather(rounded, "col", axis=1, tiled=True)
        moved = lax.all_to_all(whole, "row", split_axis=1, concat_axis=0, tiled=True)
        solved = lax.psum_scatter(
            sum_terms(moved, inv_upper[section]).astype(jnp.bfloat16),
            "row",
            scatter_dimension=0,
            tiled=True,
        ).astype(jnp.float32)
        solutions[section] = solved
        if section > 0:
            pair_index = np.array(
                [section * (section - 1) // 2 + tile for tile in range(section)], dtype=np.int32
            )
            projections = jnp.einsum(
                "nw,mwr->mnr",
                solved.astype(jnp.bfloat16),
                up_right[pair_index],
                preferred_element_type=jnp.float32,
            )
            leading = lax.psum(projections[-1:].astype(jnp.bfloat16), "col").astype(jnp.float32)
            if section > 1:
                remaining = lax.psum(projections[:-1].astype(jnp.bfloat16), "col").astype(
                    jnp.float32
                )
                summed = jnp.concatenate([remaining, leading], axis=0)
            else:
                summed = leading
            masked = (summed * rank_mask(up_ranks, pair_index, rank_cols)[:, None, :]).astype(
                jnp.bfloat16
            )
            update = jnp.einsum(
                "mnr,mwr->mnw", masked, up_left[pair_index], preferred_element_type=jnp.float32
            )
            state = state.at[:section].add(-update)
    return jnp.stack(solutions)


def solution(mesh):
    in_specs = (
        P(None, "row", "col"),
        P(None, "col", None),
        P(None, "col", None),
        P(None, "col", None),
        P(None, "col", None),
        P(),
        P(),
        P(None, "col", "row"),
        P(None, "col", "row"),
    )
    out_specs = P(None, "row", "col")
    return jax.shard_map(shards, mesh=mesh, in_specs=in_specs, out_specs=out_specs, check_vma=False)
```

profile of v0, /device:TPU:0, one launch (start us, length us, event | category | flops | bytes accessed | tf_op | source)
XLA Modules:
  0.0 1013.5 jit_solution(5519528377490401830)
XLA Ops:
  8.5 29.9 %all-gather.18.cloned.1.call-done = bf16[1,128,4096]{1,2,0:T(8,128)(2,1)} async-done(((bf16[1,128,1024]{1,2,0:T(8,128)(2,1)}), bf16[1,128,4096]{1,2,0:T(8,128)(2,1)}) %all-gather.18.cloned.1.call-update) | async-done | bytes 1048592 | tf_op jit(solution)/shard_map/all_gather | solution.py:34
  38.4 31.2 %all_to_all.152 = bf16[128,8,512]{0,2,1:T(8,128)(2,1)S(1)} all-to-all(bf16[128,8,512]{0,2,1:T(8,128)(2,1)} %bitcast.171), channel_id=1, replica_groups=mesh['row'=8,'col'=4] {'row'}, dimensions={1} | all-to-all | bytes 2097152 | tf_op jit(solution)/shard_map/all_to_all | solution.py:35
  76.8 31.4 %reduce-scatter.9.cloned.1.call-done = bf16[128,1024]{1,0:T(8,128)(2,1)} async-done(((bf16[1024,1024]{1,0:T(8,128)(2,1)}), bf16[128,1024]{1,0:T(8,128)(2,1)}) %reduce-scatter.9.cloned.1.call-update) | async-done | bytes 262160 | tf_op jit(solution)/shard_map/reduce_scatter | solution.py:36
  154.2 26.6 %all-gather.20.cloned.1.call-done = bf16[1,128,4096]{2,1,0:T(8,128)(2,1)} async-done(((bf16[1,128,1024]{2,1,0:T(8,128)(2,1)}), bf16[1,128,4096]{2,1,0:T(8,128)(2,1)}) %all-gather.20.cloned.1.call-update) | async-done | bytes 1048592 | tf_op jit(solution)/shard_map/all_gather | solution.py:34
  182.8 31.0 %all_to_all.153 = bf16[128,8,512]{2,0,1:T(8,128)(2,1)S(1)} all-to-all(bf16[128,8,512]{2,0,1:T(8,128)(2,1)S(1)} %copy.61), channel_id=1, replica_groups=mesh['row'=8,'col'=4] {'row'}, dimensions={1} | all-to-all | bytes 2097152 | tf_op jit(solution)/shard_map/all_to_all | solution.py:35
  220.9 30.8 %reduce-scatter.11.cloned.1.call-done = bf16[128,1024]{1,0:T(8,128)(2,1)} async-done(((bf16[1024,1024]{1,0:T(8,128)(2,1)}), bf16[128,1024]{1,0:T(8,128)(2,1)}) %reduce-scatter.11.cloned.1.call-update) | async-done | bytes 262160 | tf_op jit(solution)/shard_map/reduce_scatter | solution.py:36
  255.9 39.0 %all-reduce.13.cloned.1.call-done = (bf16[1,128,128]{1,2,0:T(8,128)(2,1)}, bf16[1,128,128]{1,2,0:T(8,128)(2,1)}) async-done(((bf16[1,128,128]{1,2,0:T(8,128)(2,1)}, bf16[1,128,128]{1,2,0:T(8,128)(2,1)}), (bf16[1,128,128]{1,2,0:T(8,128)(2,1)}, bf16[1,128,128]{1,2,0:T(8,128)(2,1)})) %all-reduce.13.cloned.1.call-update) | async-done | bytes 65552 | tf_op jit(solution)/shard_map/psum | solution.py:56
  297.0 26.6 %all-gather.22.cloned.1.call-done = bf16[1,128,4096]{2,1,0:T(8,128)(2,1)} async-done(((bf16[1,128,1024]{2,1,0:T(8,128)(2,1)}), bf16[1,128,4096]{2,1,0:T(8,128)(2,1)}) %all-gather.22.cloned.1.call-update) | async-done | bytes 1048592 | tf_op jit(solution)/shard_map/all_gather | solution.py:34
  325.5 31.0 %all_to_all.154 = bf16[128,8,512]{2,0,1:T(8,128)(2,1)S(1)} all-to-all(bf16[128,8,512]{2,0,1:T(8,128)(2,1)S(1)} %copy.64), channel_id=1, replica_groups=mesh['row'=8,'col'=4] {'row'}, dimensions={1} | all-to-all | bytes 2097152 | tf_op jit(solution)/shard_map/all_to_all | solution.py:35
  361.6 32.9 %reduce-scatter.13.cloned.1.call-done = bf16[128,1024]{1,0:T(8,128)(2,1)} async-done(((bf16[1024,1024]{1,0:T(8,128)(2,1)}), bf16[128,1024]{1,0:T(8,128)(2,1)}) %reduce-scatter.13.cloned.1.call-update) | async-done | bytes 262160 | tf_op jit(solution)/shard_map/reduce_scatter | solution.py:36
  438.9 31.0 %all_to_all.155 = bf16[128,8,512]{2,0,1:T(8,128)(2,1)S(1)} all-to-all(bf16[128,8,512]{2,0,1:T(8,128)(2,1)S(1)} %copy.65), channel_id=1, replica_groups=mesh['row'=8,'col'=4] {'row'}, dimensions={1} | all-to-all | bytes 2097152 | tf_op jit(solution)/shard_map/all_to_all | solution.py:35
  473.8 34.1 %reduce-scatter.15.cloned.1.call-done = bf16[128,1024]{1,0:T(8,128)(2,1)} async-done(((bf16[1024,1024]{1,0:T(8,128)(2,1)}), bf16[128,1024]{1,0:T(8,128)(2,1)}) %reduce-scatter.15.cloned.1.call-update) | async-done | bytes 262160 | tf_op jit(solution)/shard_map/reduce_scatter | solution.py:36
  508.0 26.8 %all-gather.16.cloned.1.call-done = bf16[128,4096]{1,0:T(8,128)(2,1)} async-done(((bf16[128,1024]{1,0:T(8,128)(2,1)}), bf16[128,4096]{1,0:T(8,128)(2,1)}) %all-gather.16.cloned.1.call-update) | async-done | bytes 1048592 | tf_op jit(solution)/shard_map/all_gather | solution.py:73
  536.1 31.0 %all_to_all.156 = bf16[128,8,512]{2,0,1:T(8,128)(2,1)S(1)} all-to-all(bf16[128,8,512]{2,0,1:T(8,128)(2,1)S(1)} %bitcast.165), channel_id=1, replica_groups=mesh['row'=8,'col'=4] {'row'}, dimensions={1} | all-to-all | bytes 2097152 | tf_op jit(solution)/shard_map/all_to_all | solution.py:74
  573.8 31.4 %reduce-scatter.17.cloned.1.call-done = bf16[128,1024]{1,0:T(8,128)(2,1)} async-done(((bf16[1024,1024]{1,0:T(8,128)(2,1)}), bf16[128,1024]{1,0:T(8,128)(2,1)}) %reduce-scatter.17.cloned.1.call-update) | async-done | bytes 262160 | tf_op jit(solution)/shard_map/reduce_scatter | solution.py:75
  650.6 26.6 %all-gather.26.cloned.1.call-done = bf16[1,128,4096]{2,1,0:T(8,128)(2,1)} async-done(((bf16[1,128,1024]{2,1,0:T(8,128)(2,1)}), bf16[1,128,4096]{2,1,0:T(8,128)(2,1)}) %all-gather.26.cloned.1.call-update) | async-done | bytes 1048592 | tf_op jit(solution)/shard_map/all_gather | solution.py:73
  679.1 31.0 %all_to_all.157 = bf16[128,8,512]{2,0,1:T(8,128)(2,1)S(1)} all-to-all(bf16[128,8,512]{2,0,1:T(8,128)(2,1)S(1)} %copy.69), channel_id=1, replica_groups=mesh['row'=8,'col'=4] {'row'}, dimensions={1} | all-to-all | bytes 2097152 | tf_op jit(solution)/shard_map/all_to_all | solution.py:74
  717.3 30.9 %reduce-scatter.19.cloned.1.call-done = bf16[128,1024]{1,0:T(8,128)(2,1)} async-done(((bf16[1024,1024]{1,0:T(8,128)(2,1)}), bf16[128,1024]{1,0:T(8,128)(2,1)}) %reduce-scatter.19.cloned.1.call-update) | async-done | bytes 262160 | tf_op jit(solution)/shard_map/reduce_scatter | solution.py:75
  752.3 39.0 %all-reduce.11.cloned.1.call-done = (bf16[1,128,128]{1,2,0:T(8,128)(2,1)}, bf16[1,128,128]{1,2,0:T(8,128)(2,1)}) async-done(((bf16[1,128,128]{1,2,0:T(8,128)(2,1)}, bf16[1,128,128]{1,2,0:T(8,128)(2,1)}), (bf16[1,128,128]{1,2,0:T(8,128)(2,1)}, bf16[1,128,128]{1,2,0:T(8,128)(2,1)})) %all-reduce.11.cloned.1.call-update) | async-done | bytes 65552 | tf_op jit(solution)/shard_map/psum | solution.py:92
  793.3 26.6 %all-gather.28.cloned.1.call-done = bf16[1,128,4096]{2,1,0:T(8,128)(2,1)} async-done(((bf16[1,128,1024]{2,1,0:T(8,128)(2,1)}), bf16[1,128,4096]{2,1,0:T(8,128)(2,1)}) %all-gather.28.cloned.1.call-update) | async-done | bytes 1048592 | tf_op jit(solution)/shard_map/all_gather | solution.py:73
  821.8 31.0 %all_to_all.158 = bf16[128,8,512]{2,0,1:T(8,128)(2,1)S(1)} all-to-all(bf16[128,8,512]{2,0,1:T(8,128)(2,1)S(1)} %copy.72), channel_id=1, replica_groups=mesh['row'=8,'col'=4] {'row'}, dimensions={1} | all-to-all | bytes 2097152 | tf_op jit(solution)/shard_map/all_to_all | solution.py:74
  856.7 34.1 %reduce-scatter.21.cloned.1.call-done = bf16[128,1024]{1,0:T(8,128)(2,1)} async-done(((bf16[1024,1024]{1,0:T(8,128)(2,1)}), bf16[128,1024]{1,0:T(8,128)(2,1)}) %reduce-scatter.21.cloned.1.call-update) | async-done | bytes 262160 | tf_op jit(solution)/shard_map/reduce_scatter | solution.py:75
  935.1 31.0 %all_to_all.159 = bf16[128,8,512]{2,0,1:T(8,128)(2,1)S(1)} all-to-all(bf16[128,8,512]{2,0,1:T(8,128)(2,1)S(1)} %copy.73), channel_id=1, replica_groups=mesh['row'=8,'col'=4] {'row'}, dimensions={1} | all-to-all | bytes 2097152 | tf_op jit(solution)/shard_map/all_to_all | solution.py:74
  970.0 34.2 %reduce-scatter.23.cloned.1.call-done = bf16[128,1024]{1,0:T(8,128)(2,1)} async-done(((bf16[1024,1024]{1,0:T(8,128)(2,1)}), bf16[128,1024]{1,0:T(8,128)(2,1)}) %reduce-scatter.23.cloned.1.call-update) | async-done | bytes 262160 | tf_op jit(solution)/shard_map/reduce_scatter | solution.py:75
  (154 shorter events, 250.0 us)
Async XLA Ops:
  6.5 31.9 %all-gather.18.cloned.1.call-start = ((), (), s32[]{:S(2)}) async-start(), calls=%async_computation.27 | async-start | bytes 1310720 | tf_op jit(solution)/shard_map/all_gather | solution.py:34
  8.5 99.7 %reduce-scatter.9.cloned.1.call-start = ((), (), s32[]{:S(2)}) async-start(), calls=%async_computation.16 | async-start | bytes 2359296 | tf_op jit(solution)/shard_map/reduce_scatter | solution.py:36
  74.0 77.5 %all-reduce.7.cloned.1.call-start = ((), (), s32[]{:S(2)}) async-start(), calls=%async_computation.17 | async-start | bytes 131072 | tf_op jit(solution)/shard_map/psum | solution.py:56
  76.1 34.2 %copy-start.4 = (bf16[6,1024,128]{2,1,0:T(8,128)(2,1)S(1)}, bf16[6,1024,128]{2,1,0:T(8,128)(2,1)}, u32[]{:S(2)}) copy-start(bf16[6,1024,128]{2,1,0:T(8,128)(2,1)} %param.46) | copy-start | bytes 4718596
  110.2 70.6 %all-gather.20.cloned.1.call-start = ((), (), s32[]{:S(2)}) async-start(), calls=%async_computation.28 | async-start | bytes 1310720 | tf_op jit(solution)/shard_map/all_gather | solution.py:34
  154.2 97.6 %reduce-scatter.11.cloned.1.call-start = ((), (), s32[]{:S(2)}) async-start(), calls=%async_computation.18 | async-start | bytes 2359296 | tf_op jit(solution)/shard_map/reduce_scatter | solution.py:36
  217.6 77.3 %all-reduce.13.cloned.1.call-start = ((), (), s32[]{:S(2)}) async-start(), calls=%async_computation.35 | async-start | bytes 131072 | tf_op jit(solution)/shard_map/psum | solution.py:56
  253.7 69.8 %all-gather.22.cloned.1.call-start = ((), (), s32[]{:S(2)}) async-start(), calls=%async_computation.29 | async-start | bytes 1310720 | tf_op jit(solution)/shard_map/all_gather | solution.py:34
  296.9 97.6 %reduce-scatter.13.cloned.1.call-start = ((), (), s32[]{:S(2)}) async-start(), calls=%async_computation.19 | async-start | bytes 2359296 | tf_op jit(solution)/shard_map/reduce_scatter | solution.py:36
  360.3 76.7 %all-gather.24.cloned.1.call-start = ((), (), s32[]{:S(2)}) async-start(), calls=%async_computation.30 | async-start | bytes 1310720 | tf_op jit(solution)/shard_map/all_gather | solution.py:34
  413.9 94.0 %reduce-scatter.15.cloned.1.call-start = ((), (), s32[]{:S(2)}) async-start(), calls=%async_computation.20 | async-start | bytes 2359296 | tf_op jit(solution)/shard_map/reduce_scatter | solution.py:36
  473.8 61.0 %all-gather.16.cloned.1.call-start = ((), (), s32[]{:S(2)}) async-start(), calls=%async_computation.21 | async-start | bytes 1310720 | tf_op jit(solution)/shard_map/all_gather | solution.py:73
  508.0 97.2 %reduce-scatter.17.cloned.1.call-start = ((), (), s32[]{:S(2)}) async-start(), calls=%async_computation.22 | async-start | bytes 2359296 | tf_op jit(solution)/shard_map/reduce_scatter | solution.py:75
  571.0 77.4 %all-reduce.9.cloned.1.call-start = ((), (), s32[]{:S(2)}) async-start(), calls=%async_computation.23 | async-start | bytes 131072 | tf_op jit(solution)/shard_map/psum | solution.py:94
  573.1 75.3 %copy-start.9 = (bf16[128,1024]{1,0:T(8,128)(2,1)S(1)}, bf16[128,1024]{1,0:T(8,128)(2,1)}, u32[]{:S(2)}) copy-start(bf16[128,1024]{1,0:T(8,128)(2,1)} %reduce-scatter.11.cloned.1.call-done) | copy-start | bytes 786436
  573.1 75.3 %copy-start.10 = (bf16[128,1024]{1,0:T(8,128)(2,1)S(1)}, bf16[128,1024]{1,0:T(8,128)(2,1)}, u32[]{:S(2)}) copy-start(bf16[128,1024]{1,0:T(8,128)(2,1)} %reduce-scatter.13.cloned.1.call-done) | copy-start | bytes 786436
  573.1 75.3 %copy-start.11 = (bf16[128,1024]{1,0:T(8,128)(2,1)S(1)}, bf16[128,1024]{1,0:T(8,128)(2,1)}, u32[]{:S(2)}) copy-start(bf16[128,1024]{1,0:T(8,128)(2,1)} %reduce-scatter.9.cloned.1.call-done) | copy-start | bytes 786436
  607.2 70.0 %all-gather.26.cloned.1.call-start = ((), (), s32[]{:S(2)}) async-start(), calls=%async_computation.31 | async-start | bytes 1310720 | tf_op jit(solution)/shard_map/all_gather | solution.py:73
  650.5 97.6 %reduce-scatter.19.cloned.1.call-start = ((), (), s32[]{:S(2)}) async-start(), calls=%async_computation.24 | async-start | bytes 2359296 | tf_op jit(solution)/shard_map/reduce_scatter | solution.py:75
  713.9 77.3 %all-reduce.11.cloned.1.call-start = ((), (), s32[]{:S(2)}) async-start(), calls=%async_computation.34 | async-start | bytes 131072 | tf_op jit(solution)/shard_map/psum | solution.py:92
  750.1 69.8 %all-gather.28.cloned.1.call-start = ((), (), s32[]{:S(2)}) async-start(), calls=%async_computation.32 | async-start | bytes 1310720 | tf_op jit(solution)/shard_map/all_gather | solution.py:73
  793.2 97.6 %reduce-scatter.21.cloned.1.call-start = ((), (), s32[]{:S(2)}) async-start(), calls=%async_computation.25 | async-start | bytes 2359296 | tf_op jit(solution)/shard_map/reduce_scatter | solution.py:75
  856.6 76.6 %all-gather.30.cloned.1.call-start = ((), (), s32[]{:S(2)}) async-start(), calls=%async_computation.33 | async-start | bytes 1310720 | tf_op jit(solution)/shard_map/all_gather | solution.py:73
  910.1 94.0 %reduce-scatter.23.cloned.1.call-start = ((), (), s32[]{:S(2)}) async-start(), calls=%async_computation.26 | async-start | bytes 2359296 | tf_op jit(solution)/shard_map/reduce_scatter | solution.py:75
  (12 other events, 146.6 us)
Sparse Core Ops, SparseCore 0:
  9.2 29.2 all-gather.17
  74.1 34.0 reduce-scatter.8
  111.1 40.3 all-reduce.6
  154.3 26.4 all-gather.19
  217.7 34.0 reduce-scatter.10
  254.5 40.4 all-reduce.12
  297.0 26.4 all-gather.21
  360.4 34.0 reduce-scatter.12
  414.1 22.9 all-gather.23
  473.9 34.0 reduce-scatter.14
  509.8 24.9 all-gather.15
  571.1 34.0 reduce-scatter.16
  608.0 40.3 all-reduce.8
  650.7 26.4 all-gather.25
  714.1 34.0 reduce-scatter.18
  750.8 40.3 all-reduce.10
  793.3 26.4 all-gather.27
  856.8 34.0 reduce-scatter.20
  910.3 22.8 all-gather.29
  970.1 34.0 reduce-scatter.22
where the time goes:
time: 1020 us; the launch traced here: 1010 us
  waiting for transfers between devices  596 us (58%)
  blocking collectives  313 us (31%)
  matrix products  47.9 us (5%)
  local copies, waits for them, and re-layouts  38.9 us (4%)
  between operations  14.7 us (1%)
    all_to_all x8, blocking collectives, shards(): lax.all_to_all(whole, 'row', split_axis=1, concat_axis=0, tiled=True)  248 us
    all_gather x8, waiting for transfers between devices, shards(): whole = lax.all_gather(rounded, 'col', axis=1, tiled=True)  209 us
    reduce_scatter x4, waiting for transfers between devices, shards(): lax.psum_scatter(sum_terms(moved, inv_upper[section]).astype(jnp.bfloat16...  130 us
    reduce_scatter x4, waiting for transfers between devices, shards(): lax.psum_scatter(sum_terms(moved, inv_lower[section]).astype(jnp.bfloat16...  129 us
    psum x2, waiting for transfers between devices, shards(): lax.psum(projections[1:].astype(jnp.bfloat16), 'col').astype(jnp.float32)  63.3 us
    psum x1, waiting for transfers between devices, shards(): lax.psum(projections[-1:].astype(jnp.bfloat16), 'col').astype(jnp.float32)  39 us
    psum x2, blocking collectives, shards(): lax.psum(projections[-1:].astype(jnp.bfloat16), 'col').astype(jnp.float32)  32.5 us
    psum x2, blocking collectives, shards(): lax.psum(projections[:1].astype(jnp.bfloat16), 'col').astype(jnp.float32)  32.4 us
  transfers between devices with their start and end apart: 20, of which 20 were waited for; matrix products, arithmetic and copies ran while one was open for 1% of the time, Pallas kernels for 0%

commit v1 on v0

--- a/solution.py
+++ b/solution.py
@@ -1,10 +1,21 @@
+import functools
 import jax
 import jax.numpy as jnp
 import numpy as np
 from jax import lax
 from jax.sharding import PartitionSpec as P
+from jax.lax import all_gather
 
 RBLK = 32
+
+
+def create_the_teams(tile_in, d0):
+    prior = all_gather(tile_in, "col")
+    e_now = jnp.concatenate(prior, d0)
+    return e_now
+
+
+_register_loads = functools.partial(create_the_teams, d0=1)
 
 
 def rank_mask(ranks, pair_index, rank_cols):
@@ -31,7 +42,7 @@
     forward = []
     for section in range(tile_count):
         rounded = residual[section].astype(jnp.bfloat16)
-        whole = lax.all_gather(rounded, "col", axis=1, tiled=True)
+        whole = _register_loads(rounded)
         moved = lax.all_to_all(whole, "row", split_axis=1, concat_axis=0, tiled=True)
         solved = lax.psum_scatter(
             sum_terms(moved, inv_lower[section]).astype(jnp.bfloat16),

time: 1020 us -> 1020 us (level)
    all_gather x0 -> x4, waiting for transfers between devices: none -> 106 us  [create_the_teams(): prior = all_gather(tile_in, 'col')]
    all_gather x8 -> x4, waiting for transfers between devices: 209 us -> 103 us  [shards(): whole = lax.all_gather(rounded, 'col', axis=1, tiled=True)]
  transfers between devices with their start and end apart: 20 -> 20, of which waited for: 20 -> 20; matrix products, arithmetic and copies ran while one was open for 1% -> 2% of each run, Pallas kernels for 0% -> 0%
where the time goes in v1:
time: 1020 us
  waiting for transfers between devices  593 us (58%)
  blocking collectives  313 us (31%)
  matrix products  47.9 us (5%)
  local copies, waits for them, and re-layouts  44.8 us (4%)
  between operations  14.8 us (1%)
    all_to_all x8, blocking collectives, shards(): lax.all_to_all(whole, 'row', split_axis=1, concat_axis=0, tiled=True)  248 us
    reduce_scatter x4, waiting for transfers between devices, shards(): lax.psum_scatter(sum_terms(moved, inv_upper[section]).astype(jnp.bfloat16...  130 us
    reduce_scatter x4, waiting for transfers between devices, shards(): lax.psum_scatter(sum_terms(moved, inv_lower[section]).astype(jnp.bfloat16...  129 us
    all_gather x4, waiting for transfers between devices, create_the_teams(): prior = all_gather(tile_in, 'col')  106 us
    all_gather x4, waiting for transfers between devices, shards(): whole = lax.all_gather(rounded, 'col', axis=1, tiled=True)  103 us
    psum x2, waiting for transfers between devices, shards(): lax.psum(projections[1:].astype(jnp.bfloat16), 'col').astype(jnp.float32)  61.9 us
    psum x1, waiting for transfers between devices, shards(): lax.psum(projections[-1:].astype(jnp.bfloat16), 'col').astype(jnp.float32)  39 us
    psum x2, blocking collectives, shards(): lax.psum(projections[:1].astype(jnp.bfloat16), 'col').astype(jnp.float32)  32.5 us
  transfers between devices with their start and end apart: 20, of which 20 were waited for; matrix products, arithmetic and copies ran while one was open for 2% of the time, Pallas kernels for 0%

profile of v1, /device:TPU:0, one launch (start us, length us, event | category | flops | bytes accessed | tf_op | source)
XLA Modules:
  0.0 1016.8 jit_solution(6012802520915342633)
XLA Ops:
  8.4 30.0 %all-gather.12.cloned.1.call-done = bf16[4,128,1024]{2,1,0:T(8,128)(2,1)} async-done(((bf16[1,128,1024]{2,1,0:T(8,128)(2,1)}), bf16[4,128,1024]{2,1,0:T(8,128)(2,1)}) %all-gather.12.cloned.1.call-update) | async-done | bytes 1048592 | tf_op jit(solution)/shard_map/all_gather | solution.py:13
  40.0 31.0 %all_to_all.152 = bf16[128,8,512]{0,2,1:T(8,128)(2,1)S(1)} all-to-all(bf16[128,8,512]{0,2,1:T(8,128)(2,1)S(1)} %bitcast.160), channel_id=1, replica_groups=mesh['row'=8,'col'=4] {'row'}, dimensions={1} | all-to-all | bytes 2097152 | tf_op jit(solution)/shard_map/all_to_all | solution.py:46
  78.2 31.4 %reduce-scatter.9.cloned.1.call-done = bf16[128,1024]{1,0:T(8,128)(2,1)} async-done(((bf16[1024,1024]{1,0:T(8,128)(2,1)}), bf16[128,1024]{1,0:T(8,128)(2,1)}) %reduce-scatter.9.cloned.1.call-update) | async-done | bytes 262160 | tf_op jit(solution)/shard_map/reduce_scatter | solution.py:47
  155.6 26.6 %all-gather.14.cloned.1.call-done = bf16[4,128,1024]{2,1,0:T(8,128)(2,1)} async-done(((bf16[1,128,1024]{2,1,0:T(8,128)(2,1)}), bf16[4,128,1024]{2,1,0:T(8,128)(2,1)}) %all-gather.14.cloned.1.call-update) | async-done | bytes 1048592 | tf_op jit(solution)/shard_map/all_gather | solution.py:13
  183.9 31.1 %all_to_all.153 = bf16[128,8,512]{0,2,1:T(8,128)(2,1)} all-to-all(bf16[128,8,512]{0,2,1:T(8,128)(2,1)S(1)} %bitcast.162), channel_id=1, replica_groups=mesh['row'=8,'col'=4] {'row'}, dimensions={1} | all-to-all | bytes 2097152 | tf_op jit(solution)/shard_map/all_to_all | solution.py:46
  223.6 30.8 %reduce-scatter.11.cloned.1.call-done = bf16[128,1024]{1,0:T(8,128)(2,1)} async-done(((bf16[1024,1024]{1,0:T(8,128)(2,1)}), bf16[128,1024]{1,0:T(8,128)(2,1)}) %reduce-scatter.11.cloned.1.call-update) | async-done | bytes 262160 | tf_op jit(solution)/shard_map/reduce_scatter | solution.py:47
  258.6 39.1 %all-reduce.13.cloned.1.call-done = (bf16[1,128,128]{1,2,0:T(8,128)(2,1)}, bf16[1,128,128]{1,2,0:T(8,128)(2,1)}) async-done(((bf16[1,128,128]{1,2,0:T(8,128)(2,1)}, bf16[1,128,128]{1,2,0:T(8,128)(2,1)}), (bf16[1,128,128]{1,2,0:T(8,128)(2,1)}, bf16[1,128,128]{1,2,0:T(8,128)(2,1)})) %all-reduce.13.cloned.1.call-update) | async-done | bytes 65552 | tf_op jit(solution)/shard_map/psum | solution.py:67
  299.7 26.6 %all-gather.16.cloned.1.call-done = bf16[4,128,1024]{2,1,0:T(8,128)(2,1)} async-done(((bf16[1,128,1024]{2,1,0:T(8,128)(2,1)}), bf16[4,128,1024]{2,1,0:T(8,128)(2,1)}) %all-gather.16.cloned.1.call-update) | async-done | bytes 1048592 | tf_op jit(solution)/shard_map/all_gather | solution.py:13
  328.0 31.0 %all_to_all.154 = bf16[128,8,512]{0,2,1:T(8,128)(2,1)S(1)} all-to-all(bf16[128,8,512]{0,2,1:T(8,128)(2,1)S(1)} %bitcast.164), channel_id=1, replica_groups=mesh['row'=8,'col'=4] {'row'}, dimensions={1} | all-to-all | bytes 2097152 | tf_op jit(solution)/shard_map/all_to_all | solution.py:46
  364.8 32.8 %reduce-scatter.13.cloned.1.call-done = bf16[128,1024]{1,0:T(8,128)(2,1)} async-done(((bf16[1024,1024]{1,0:T(8,128)(2,1)}), bf16[128,1024]{1,0:T(8,128)(2,1)}) %reduce-scatter.13.cloned.1.call-update) | async-done | bytes 262160 | tf_op jit(solution)/shard_map/reduce_scatter | solution.py:47
  441.7 31.0 %all_to_all.155 = bf16[128,8,512]{0,2,1:T(8,128)(2,1)S(1)} all-to-all(bf16[128,8,512]{0,2,1:T(8,128)(2,1)S(1)} %bitcast.166), channel_id=1, replica_groups=mesh['row'=8,'col'=4] {'row'}, dimensions={1} | all-to-all | bytes 2097152 | tf_op jit(solution)/shard_map/all_to_all | solution.py:46
  477.1 34.1 %reduce-scatter.15.cloned.1.call-done = bf16[128,1024]{1,0:T(8,128)(2,1)} async-done(((bf16[1024,1024]{1,0:T(8,128)(2,1)}), bf16[128,1024]{1,0:T(8,128)(2,1)}) %reduce-scatter.15.cloned.1.call-update) | async-done | bytes 262160 | tf_op jit(solution)/shard_map/reduce_scatter | solution.py:47
  511.3 26.8 %all-gather.20.cloned.1.call-done = bf16[128,4096]{1,0:T(8,128)(2,1)} async-done(((bf16[128,1024]{1,0:T(8,128)(2,1)}), bf16[128,4096]{1,0:T(8,128)(2,1)}) %all-gather.20.cloned.1.call-update) | async-done | bytes 1048592 | tf_op jit(solution)/shard_map/all_gather | solution.py:84
  539.4 31.0 %all_to_all.156 = bf16[128,8,512]{2,0,1:T(8,128)(2,1)S(1)} all-to-all(bf16[128,8,512]{2,0,1:T(8,128)(2,1)S(1)} %bitcast.168), channel_id=1, replica_groups=mesh['row'=8,'col'=4] {'row'}, dimensions={1} | all-to-all | bytes 2097152 | tf_op jit(solution)/shard_map/all_to_all | solution.py:85
  577.0 31.4 %reduce-scatter.17.cloned.1.call-done = bf16[128,1024]{1,0:T(8,128)(2,1)} async-done(((bf16[1024,1024]{1,0:T(8,128)(2,1)}), bf16[128,1024]{1,0:T(8,128)(2,1)}) %reduce-scatter.17.cloned.1.call-update) | async-done | bytes 262160 | tf_op jit(solution)/shard_map/reduce_scatter | solution.py:86
  653.9 26.6 %all-gather.22.cloned.1.call-done = bf16[1,128,4096]{2,1,0:T(8,128)(2,1)} async-done(((bf16[1,128,1024]{2,1,0:T(8,128)(2,1)}), bf16[1,128,4096]{2,1,0:T(8,128)(2,1)}) %all-gather.22.cloned.1.call-update) | async-done | bytes 1048592 | tf_op jit(solution)/shard_map/all_gather | solution.py:84
  682.4 31.0 %all_to_all.157 = bf16[128,8,512]{2,0,1:T(8,128)(2,1)S(1)} all-to-all(bf16[128,8,512]{2,0,1:T(8,128)(2,1)S(1)} %copy.77), channel_id=1, replica_groups=mesh['row'=8,'col'=4] {'row'}, dimensions={1} | all-to-all | bytes 2097152 | tf_op jit(solution)/shard_map/all_to_all | solution.py:85
  720.6 30.8 %reduce-scatter.19.cloned.1.call-done = bf16[128,1024]{1,0:T(8,128)(2,1)} async-done(((bf16[1024,1024]{1,0:T(8,128)(2,1)}), bf16[128,1024]{1,0:T(8,128)(2,1)}) %reduce-scatter.19.cloned.1.call-update) | async-done | bytes 262160 | tf_op jit(solution)/shard_map/reduce_scatter | solution.py:86
  755.5 39.0 %all-reduce.11.cloned.1.call-done = (bf16[1,128,128]{1,2,0:T(8,128)(2,1)}, bf16[1,128,128]{1,2,0:T(8,128)(2,1)}) async-done(((bf16[1,128,128]{1,2,0:T(8,128)(2,1)}, bf16[1,128,128]{1,2,0:T(8,128)(2,1)}), (bf16[1,128,128]{1,2,0:T(8,128)(2,1)}, bf16[1,128,128]{1,2,0:T(8,128)(2,1)})) %all-reduce.11.cloned.1.call-update) | async-done | bytes 65552 | tf_op jit(solution)/shard_map/psum | solution.py:103
  796.6 26.6 %all-gather.24.cloned.1.call-done = bf16[1,128,4096]{2,1,0:T(8,128)(2,1)} async-done(((bf16[1,128,1024]{2,1,0:T(8,128)(2,1)}), bf16[1,128,4096]{2,1,0:T(8,128)(2,1)}) %all-gather.24.cloned.1.call-update) | async-done | bytes 1048592 | tf_op jit(solution)/shard_map/all_gather | solution.py:84
  825.1 31.0 %all_to_all.158 = bf16[128,8,512]{2,0,1:T(8,128)(2,1)S(1)} all-to-all(bf16[128,8,512]{2,0,1:T(8,128)(2,1)S(1)} %copy.80), channel_id=1, replica_groups=mesh['row'=8,'col'=4] {'row'}, dimensions={1} | all-to-all | bytes 2097152 | tf_op jit(solution)/shard_map/all_to_all | solution.py:85
  860.0 34.1 %reduce-scatter.21.cloned.1.call-done = bf16[128,1024]{1,0:T(8,128)(2,1)} async-done(((bf16[1024,1024]{1,0:T(8,128)(2,1)}), bf16[128,1024]{1,0:T(8,128)(2,1)}) %reduce-scatter.21.cloned.1.call-update) | async-done | bytes 262160 | tf_op jit(solution)/shard_map/reduce_scatter | solution.py:86
  938.5 31.0 %all_to_all.159 = bf16[128,8,512]{2,0,1:T(8,128)(2,1)S(1)} all-to-all(bf16[128,8,512]{2,0,1:T(8,128)(2,1)S(1)} %copy.81), channel_id=1, replica_groups=mesh['row'=8,'col'=4] {'row'}, dimensions={1} | all-to-all | bytes 2097152 | tf_op jit(solution)/shard_map/all_to_all | solution.py:85
  973.3 34.2 %reduce-scatter.23.cloned.1.call-done = bf16[128,1024]{1,0:T(8,128)(2,1)} async-done(((bf16[1024,1024]{1,0:T(8,128)(2,1)}), bf16[128,1024]{1,0:T(8,128)(2,1)}) %reduce-scatter.23.cloned.1.call-update) | async-done | bytes 262160 | tf_op jit(solution)/shard_map/reduce_scatter | solution.py:86
  (150 shorter events, 253.1 us)
Async XLA Ops:
  6.5 31.9 %all-gather.12.cloned.1.call-start = ((), (), s32[]{:S(2)}) async-start(), calls=%async_computation.16 | async-start | bytes 1310720 | tf_op jit(solution)/shard_map/all_gather | solution.py:13
  8.3 101.2 %reduce-scatter.9.cloned.1.call-start = ((), (), s32[]{:S(2)}) async-start(), calls=%async_computation.17 | async-start | bytes 2359296 | tf_op jit(solution)/shard_map/reduce_scatter | solution.py:47
  75.4 77.4 %all-reduce.7.cloned.1.call-start = ((), (), s32[]{:S(2)}) async-start(), calls=%async_computation.18 | async-start | bytes 131072 | tf_op jit(solution)/shard_map/psum | solution.py:67
  111.6 70.6 %all-gather.14.cloned.1.call-start = ((), (), s32[]{:S(2)}) async-start(), calls=%async_computation.19 | async-start | bytes 1310720 | tf_op jit(solution)/shard_map/all_gather | solution.py:13
  155.6 98.9 %reduce-scatter.11.cloned.1.call-start = ((), (), s32[]{:S(2)}) async-start(), calls=%async_computation.20 | async-start | bytes 2359296 | tf_op jit(solution)/shard_map/reduce_scatter | solution.py:47
  220.3 77.5 %all-reduce.13.cloned.1.call-start = ((), (), s32[]{:S(2)}) async-start(), calls=%async_computation.35 | async-start | bytes 131072 | tf_op jit(solution)/shard_map/psum | solution.py:67
  256.4 69.9 %all-gather.16.cloned.1.call-start = ((), (), s32[]{:S(2)}) async-start(), calls=%async_computation.21 | async-start | bytes 1310720 | tf_op jit(solution)/shard_map/all_gather | solution.py:13
  299.7 97.9 %reduce-scatter.13.cloned.1.call-start = ((), (), s32[]{:S(2)}) async-start(), calls=%async_computation.22 | async-start | bytes 2359296 | tf_op jit(solution)/shard_map/reduce_scatter | solution.py:47
  363.4 76.7 %all-gather.18.cloned.1.call-start = ((), (), s32[]{:S(2)}) async-start(), calls=%async_computation.23 | async-start | bytes 1310720 | tf_op jit(solution)/shard_map/all_gather | solution.py:13
  417.0 94.1 %reduce-scatter.15.cloned.1.call-start = ((), (), s32[]{:S(2)}) async-start(), calls=%async_computation.24 | async-start | bytes 2359296 | tf_op jit(solution)/shard_map/reduce_scatter | solution.py:47
  477.0 61.1 %all-gather.20.cloned.1.call-start = ((), (), s32[]{:S(2)}) async-start(), calls=%async_computation.25 | async-start | bytes 1310720 | tf_op jit(solution)/shard_map/all_gather | solution.py:84
  511.2 97.2 %reduce-scatter.17.cloned.1.call-start = ((), (), s32[]{:S(2)}) async-start(), calls=%async_computation.26 | async-start | bytes 2359296 | tf_op jit(solution)/shard_map/reduce_scatter | solution.py:86
  574.2 77.4 %all-reduce.9.cloned.1.call-start = ((), (), s32[]{:S(2)}) async-start(), calls=%async_computation.27 | async-start | bytes 131072 | tf_op jit(solution)/shard_map/psum | solution.py:105
  576.4 75.3 %copy-start.7 = (bf16[128,1024]{1,0:T(8,128)(2,1)S(1)}, bf16[128,1024]{1,0:T(8,128)(2,1)}, u32[]{:S(2)}) copy-start(bf16[128,1024]{1,0:T(8,128)(2,1)} %reduce-scatter.11.cloned.1.call-done) | copy-start | bytes 786436
  576.4 75.3 %copy-start.8 = (bf16[128,1024]{1,0:T(8,128)(2,1)S(1)}, bf16[128,1024]{1,0:T(8,128)(2,1)}, u32[]{:S(2)}) copy-start(bf16[128,1024]{1,0:T(8,128)(2,1)} %reduce-scatter.13.cloned.1.call-done) | copy-start | bytes 786436
  576.4 75.3 %copy-start.9 = (bf16[128,1024]{1,0:T(8,128)(2,1)S(1)}, bf16[128,1024]{1,0:T(8,128)(2,1)}, u32[]{:S(2)}) copy-start(bf16[128,1024]{1,0:T(8,128)(2,1)} %reduce-scatter.9.cloned.1.call-done) | copy-start | bytes 786436
  610.5 70.0 %all-gather.22.cloned.1.call-start = ((), (), s32[]{:S(2)}) async-start(), calls=%async_computation.31 | async-start | bytes 1310720 | tf_op jit(solution)/shard_map/all_gather | solution.py:84
  653.8 97.6 %reduce-scatter.19.cloned.1.call-start = ((), (), s32[]{:S(2)}) async-start(), calls=%async_computation.28 | async-start | bytes 2359296 | tf_op jit(solution)/shard_map/reduce_scatter | solution.py:86
  717.2 77.3 %all-reduce.11.cloned.1.call-start = ((), (), s32[]{:S(2)}) async-start(), calls=%async_computation.34 | async-start | bytes 131072 | tf_op jit(solution)/shard_map/psum | solution.py:103
  753.4 69.8 %all-gather.24.cloned.1.call-start = ((), (), s32[]{:S(2)}) async-start(), calls=%async_computation.32 | async-start | bytes 1310720 | tf_op jit(solution)/shard_map/all_gather | solution.py:84
  796.5 97.6 %reduce-scatter.21.cloned.1.call-start = ((), (), s32[]{:S(2)}) async-start(), calls=%async_computation.29 | async-start | bytes 2359296 | tf_op jit(solution)/shard_map/reduce_scatter | solution.py:86
  859.9 76.6 %all-gather.26.cloned.1.call-start = ((), (), s32[]{:S(2)}) async-start(), calls=%async_computation.33 | async-start | bytes 1310720 | tf_op jit(solution)/shard_map/all_gather | solution.py:84
  913.5 94.0 %reduce-scatter.23.cloned.1.call-start = ((), (), s32[]{:S(2)}) async-start(), calls=%async_computation.30 | async-start | bytes 2359296 | tf_op jit(solution)/shard_map/reduce_scatter | solution.py:86
  973.3 34.2 %copy-start.6 = (bf16[128,1024]{1,0:T(8,128)(2,1)S(1)}, bf16[128,1024]{1,0:T(8,128)(2,1)}, u32[]{:S(2)}) copy-start(bf16[128,1024]{1,0:T(8,128)(2,1)} %reduce-scatter.17.cloned.1.call-done) | copy-start | bytes 786436
  (10 other events, 78.2 us)
Sparse Core Ops, SparseCore 0:
  9.2 29.2 all-gather.11
  75.5 34.0 reduce-scatter.8
  112.4 40.3 all-reduce.6
  155.7 26.4 all-gather.13
  220.4 34.0 reduce-scatter.10
  257.2 40.5 all-reduce.12
  299.8 26.4 all-gather.15
  363.5 34.0 reduce-scatter.12
  417.2 22.8 all-gather.17
  477.1 34.0 reduce-scatter.14
  513.0 25.0 all-gather.19
  574.4 34.0 reduce-scatter.16
  611.3 40.3 all-reduce.8
  653.9 26.4 all-gather.21
  717.4 34.0 reduce-scatter.18
  754.1 40.4 all-reduce.10
  796.7 26.4 all-gather.23
  860.1 34.0 reduce-scatter.20
  913.6 22.8 all-gather.25
  973.4 34.0 reduce-scatter.22
